TPU v7x, 128 devices: a whole 4x4x4 slice. The times are simulated.
128 devices in a mesh: dp: 16 (over x, y_hi, core), mp: 8 (over y_lo, z).
Axes of the slice: x: 4, y: 4 (y_hi: 2, y_lo: 2; y = y_hi * 2 + y_lo), z: 4, core: 2. Of those that a mesh axis runs over, the one named last changes fastest.
Arguments:
- tokens: bfloat16 [12288, 6144], P('dp', 'mp'), may hold values from -6 to 6
- ln_gain: bfloat16 [6144], P('mp'), may hold values from 0.5 to 1.5
- weights: bfloat16 [6144, 12288], P('dp', 'mp'), may hold values from -0.078125 to 0.078125
- grad_partials: bfloat16 [16, 6144, 12288], P('dp', None, 'mp'), may hold values from -40 to 40, as said below
Outputs:
- hidden: bfloat16 [12288, 12288], P('dp', 'mp')
- perturbed_weights: bfloat16 [6144, 12288], P('dp', 'mp')
Inputs may be any that keep to these rules, and one draw needn't show every extreme that they name: `grad_partials`: each slice along the first dimension is one data shard's gradient.
All inputs are finite; a program needn't handle non-finite values.
Results may differ from a plain program's by a relative error of at most 0.012.
Values may be sent and summed in bfloat16 or wider, within the bound.
A program may use at most 192 MiB of HBM per device.

v0:
```python
import functools
import math

import jax
import jax.numpy as jnp
from jax import lax
from jax.sharding import Mesh
from jax.sharding import PartitionSpec as P

FF = 12288
MP = ("mp_0", "mp_1")
DP = ("dp_0", "dp_1", "dp_2")
DP_MP = ("dp_0", "dp_1", "dp_2", "mp_0", "mp_1")


def over_axes(shard, axes):
    return functools.reduce(lax.psum, axes, shard)


def per_device(tokens, ln_gain, weights, grad_partials):
    feats, gains = (
        lax.all_gather(tokens, MP, axis=1, tiled=True),
        lax.all_gather(ln_gain, MP, axis=0, tiled=True),
    )
    values = feats.astype(jnp.float32)
    center = jnp.mean(values, axis=1, keepdims=True)
    spread = jnp.mean((values - center) ** 2, axis=1, keepdims=True)
    normed = ((values - center) / jnp.sqrt(spread + 1e-06) * gains.astype(jnp.float32)).astype(
        jnp.bfloat16
    )
    radius = 0.7 * math.sqrt(FF)
    grad_rows = lax.psum_scatter(grad_partials, DP, scatter_dimension=1, tiled=True).astype(
        jnp.float32
    )[0]
    squares = over_axes(jnp.sum(grad_rows * grad_rows), DP_MP)
    scale = radius / jnp.sqrt(squares + 1e-12)
    perturbed = (weights.astype(jnp.float32) + scale * grad_rows).astype(jnp.bfloat16)
    pre = jnp.dot(
        normed,
        lax.all_gather(perturbed, DP, axis=0, tiled=True),
        preferred_element_type=jnp.float32,
    )
    hidden = jax.nn.gelu(pre, approximate=False).astype(jnp.bfloat16)
    return (hidden, perturbed)


def solution(mesh):
    torus = Mesh(mesh.devices.reshape(4, 2, 2, 2, 4), ("dp_0", "dp_1", "dp_2", "mp_0", "mp_1"))
    placed = (P(DP, MP), P(MP), P(DP, MP), P(DP, None, MP))
    return jax.shard_map(
        per_device, mesh=torus, in_specs=placed, out_specs=(P(DP, MP), P(DP, MP)), check_vma=False
    )
```

profile of v0, /device:TPU:1, one launch (start us, length us, event | category | flops | bytes accessed | tf_op | source)
XLA Modules:
  0.0 411.7 jit_solution(105245008111856210)
XLA Ops:
  8.0 0.0 copy-start.1
  8.0 0.0 reduce-scatter.2.cloned.1.call-start
  8.1 0.7 reduce-scatter.2.cloned.1.call-update
  8.7 0.0 copy-start.2
  8.8 0.0 all-gather.4.cloned.1.call-start
  8.8 0.5 all-gather.4.cloned.1.call-update
  9.3 0.0 all-gather.6.cloned.1.call-start
  9.4 203.7 %reduce-scatter.2.cloned.1.call-done = bf16[1,384,1536]{2,1,0:T(8,128)(2,1)} async-done(((bf16[1,6144,1536]{2,1,0:T(8,128)(2,1)}), bf16[1,384,1536]{2,1,0:T(8,128)(2,1)}) %reduce-scatter.2.cloned.1.call-update) | async-done | bytes 1179664 | tf_op jit(solution)/shard_map/reduce_scatter | solution.py:32
  213.1 2.5 fusion.19
  215.5 7.2 %psum.35 = f32[]{:T(128)} all-reduce(f32[]{:T(128)} %fusion.19), channel_id=1, replica_groups=mesh['dp_0'=4,'dp_1'=2,'dp_2'=2,'mp_0'=2,'mp_1'=4] {'dp_0'}, use_global_device_ids=true, to_apply=%region_4.0 | all-reduce | flops 1 | bytes 8 | tf_op jit(solution)/shard_map/psum | solution.py:17
  222.7 5.9 %psum.36 = f32[]{:T(128)} all-reduce(f32[]{:T(128)} %psum.35), channel_id=1, replica_groups=mesh['dp_0'=4,'dp_1'=2,'dp_2'=2,'mp_0'=2,'mp_1'=4] {'dp_1'}, use_global_device_ids=true, to_apply=%region_5.0 | all-reduce | flops 1 | bytes 8 | tf_op jit(solution)/shard_map/psum | solution.py:17
  228.6 7.3 %psum.37 = f32[]{:T(128)} all-reduce(f32[]{:T(128)} %psum.36), channel_id=1, replica_groups=mesh['dp_0'=4,'dp_1'=2,'dp_2'=2,'mp_0'=2,'mp_1'=4] {'dp_2'}, use_global_device_ids=true, to_apply=%region_6.0 | all-reduce | flops 1 | bytes 8 | tf_op jit(solution)/shard_map/psum | solution.py:17
  236.0 4.4 %psum.38 = f32[]{:T(128)} all-reduce(f32[]{:T(128)} %psum.37), channel_id=1, replica_groups=mesh['dp_0'=4,'dp_1'=2,'dp_2'=2,'mp_0'=2,'mp_1'=4] {'mp_0'}, use_global_device_ids=true, to_apply=%region_7.0 | all-reduce | flops 1 | bytes 8 | tf_op jit(solution)/shard_map/psum | solution.py:17
  240.3 9.3 %psum.39 = f32[]{:T(128)} all-reduce(f32[]{:T(128)} %psum.38), channel_id=1, replica_groups=mesh['dp_0'=4,'dp_1'=2,'dp_2'=2,'mp_0'=2,'mp_1'=4] {'mp_1'}, use_global_device_ids=true, to_apply=%region_8.0 | all-reduce | flops 1 | bytes 8 | tf_op jit(solution)/shard_map/psum | solution.py:17
  250.3 0.0 copy-done.1
  250.3 2.7 fusion.22
  253.0 0.0 all-gather.6.cloned.1.call-update
  253.0 0.0 copy-done.2
  253.0 22.9 %all-gather = bf16[8,1,768]{2,1,0:T(2,128)(2,1)S(1)} all-gather(bf16[1,1,768]{2,1,0:T(2,128)(2,1)S(1)} %reshape.20), channel_id=1, replica_groups=mesh['dp_0'=4,'dp_1'=2,'dp_2'=2,'mp_0'=2,'mp_1'=4] {'mp_0','mp_1'}, dimensions={0}, use_global_device_ids=true | all-gather | bytes 13824 | tf_op jit(solution)/shard_map/all_gather | solution.py:23
  276.0 0.0 all-gather.4.cloned.1.call-done
  276.0 0.0 copy-start
  276.0 5.2 %convert_reduce_fusion = f32[768]{0:T(1024)S(1)} fusion(bf16[768,6144]{1,0:T(8,128)(2,1)} %all-gather.4.cloned.1.call-done), kind=kLoop, calls=%fused_computation.1 | loop fusion | flops 9436416 | bytes 9440256 | tf_op jit(solution)/shard_map/reduce_sum | solution.py:26
  281.3 1.4 copy-done
  282.6 2.6 fusion.2
  285.2 85.6 %all-gather.6.cloned.1.call-done = bf16[6144,1536]{1,0:T(8,128)(2,1)} async-done(((bf16[384,1536]{1,0:T(8,128)(2,1)}), bf16[6144,1536]{1,0:T(8,128)(2,1)}) %all-gather.6.cloned.1.call-update) | async-done | bytes 18874384 | tf_op jit(solution)/shard_map/all_gather | solution.py:40
  370.9 33.5 %fusion.9 = bf16[768,1536]{1,0:T(8,128)(2,1)} fusion(bf16[6144,1536]{1,0:T(8,128)(2,1)} %all-gather.6.cloned.1.call-done, bf16[768,6144]{1,0:T(8,128)(2,1)} %all-gather.4.cloned.1.call-done, f32[6144]{0:T(1024)S(1)} %bitcast.8, f32[768]{0:T(1024)S(1)} %add_sqrt_fusion, f32[768]{0:T(1024)S(1)} %broadcast_multiply_fusion), kind=kOutput, calls=%fused_computation.11 | convolution fusion | flops 14595784704 | bytes 30701568 | tf_op jit(solution)/shard_map/dot_general | solution.py:38
  (4 shorter events, 0.0 us)
Async XLA Ops:
  8.0 242.3 %copy-start.1 = (bf16[384,1536]{1,0:T(8,128)(2,1)S(1)}, bf16[384,1536]{1,0:T(8,128)(2,1)}, u32[]{:S(2)}) copy-start(bf16[384,1536]{1,0:T(8,128)(2,1)} %param.6) | copy-start | bytes 3538948
  8.0 205.1 %reduce-scatter.2.cloned.1.call-start = ((), (), s32[]{:S(2)}) async-start(), calls=%async_computation.2 | async-start | bytes 20054016 | tf_op jit(solution)/shard_map/reduce_scatter | solution.py:32
  8.7 244.3 %copy-start.2 = (bf16[768]{0:T(1024)(128)(2,1)S(1)}, bf16[768]{0:T(1024)(128)(2,1)}, u32[]{:S(2)}) copy-start(bf16[768]{0:T(1024)(128)(2,1)} %param.5) | copy-start | bytes 4612
  8.8 267.3 %all-gather.4.cloned.1.call-start = ((), (), s32[]{:S(2)}) async-start(), calls=%async_computation.1 | async-start | bytes 10616832 | tf_op jit(solution)/shard_map/all_gather | solution.py:22
  9.3 361.5 %all-gather.6.cloned.1.call-start = ((), (), s32[]{:S(2)}) async-start(), calls=%async_computation.3 | async-start | bytes 20054016 | tf_op jit(solution)/shard_map/all_gather | solution.py:40
  276.0 6.6 %copy-start = (bf16[768,6144]{1,0:T(8,128)(2,1)S(1)}, bf16[768,6144]{1,0:T(8,128)(2,1)}, u32[]{:S(2)}) copy-start(bf16[768,6144]{1,0:T(8,128)(2,1)} %all-gather.4.cloned.1.call-done) | copy-start | bytes 28311556
Sparse Core Ops, SparseCore 0:
  13.2 199.7 reduce-scatter.1
Sparse Core Ops, SparseCore 1:
  10.9 134.6 all-gather.3
  253.1 117.7 all-gather.5
where the time goes:
time: 412 us
  waiting for transfers between devices  291 us (71%)
  blocking collectives  57 us (14%)
  matrix products  33.5 us (8%)
  between operations  16.2 us (4%)
  other arithmetic  13 us (3%)
    reduce_scatter x1, waiting for transfers between devices, per_device(): lax.psum_scatter(grad_partials, DP, scatter_dimension=1, tiled=True)  204 us
    all_gather x1, waiting for transfers between devices, per_device(): lax.all_gather(perturbed, DP, axis=0, tiled=True)  85.6 us
    psum x5, blocking collectives, over_axes(): return functools.reduce(lax.psum, axes, shard)  34.1 us
    dot_general x1, matrix products, per_device(): jnp.dot(normed, lax.all_gather(perturbed, DP, axis=0, tiled=True), prefer...  33.5 us
    all_gather x1, blocking collectives, per_device(): lax.all_gather(ln_gain, MP, axis=0, tiled=True)  22.9 us
  transfers between devices with their start and end apart: 3, of which 2 were waited for; matrix products, arithmetic and copies ran while one was open for 3% of the time, Pallas kernels for 0%

commit v1 on v0

v1 whole, which is shorter than its diff:
```python
import functools
import math

import jax
import jax.numpy as jnp
from jax import lax
from jax.experimental import pallas as pl
from jax.experimental.pallas import tpu as pltpu
from jax.sharding import Mesh
from jax.sharding import PartitionSpec as P

FF = 12288
MP = ("mp_0", "mp_1")
DP = ("dp_0", "dp_1", "dp_2")
AXES = ("dp_0", "dp_1", "dp_2", "mp_0", "mp_1")
MESH = pl.DeviceIdType.MESH

BLK = 384
HALF = BLK // 2
COLS = 1536
TOK = 768
FEAT = 768
NMP = 8
D = FEAT * NMP
CH = 16
F32 = jnp.float32
BF16 = jnp.bfloat16


def kernel(
    tok_hbm, gain_hbm, w_hbm, grad_hbm, hid_hbm, pert_hbm,
    own, oth, xr, yr, tok, gb, gf, wb, pre, hid, nsend, nrecv,
    ssem, rsem, lsem,
):
    x, yh, c, yl, z = [lax.axis_index(a) for a in AXES]
    y = yh * 2 + yl

    def xid(k):
        return {"dp_0": lax.rem(x + k, 4)}

    def yid(k):
        yy = lax.rem(y + k, 4)
        return {"dp_1": yy // 2, "mp_0": lax.rem(yy, 2)}

    def zid(k):
        return {"mp_1": lax.rem(z + k, 4)}

    core = {"dp_2": 1 - c}
    ypair = {"mp_0": 1 - yl}
    yfar = {"dp_1": 1 - yh}

    count = {"s": 0, "l": 0}
    sends = []

    def remote(src, dst, dev):
        i = count["s"]
        count["s"] += 1
        cp = pltpu.make_async_remote_copy(
            src_ref=src, dst_ref=dst, send_sem=ssem.at[i], recv_sem=rsem.at[i],
            device_id=dev, device_id_type=MESH,
        )
        sends.append(cp)
        return cp

    def local(src, dst):
        i = count["l"]
        count["l"] += 1
        cp = pltpu.make_async_copy(src, dst, lsem.at[i])
        cp.start()
        return cp

    def rows(start, n):
        return pl.ds(pl.multiple_of(start, 16), n)

    def block(xk, far):
        yy = 1 - yh if far else yh
        return lax.rem(x + xk, 4) * 2 + yy

    barrier = pltpu.get_barrier_semaphore()
    peers = [core] + [xid(k) for k in (1, 2, 3)] + [yid(k) for k in (1, 2, 3)] + [zid(k) for k in (1, 2, 3)]
    for p in peers:
        pl.semaphore_signal(barrier, inc=1, device_id=p, device_id_type=MESH)
    order = [(2, True), (1, True), (3, True), (2, False), (1, False), (3, False), (0, True), (0, False)]
    mine = []
    for xk, far in order:
        j = block(xk, far)
        mine.append(local(grad_hbm.at[0, rows((2 * j + c) * BLK, BLK), :], own.at[j]))
    me_t = yl * 4 + z
    pa_t = (1 - yl) * 4 + z
    lt = local(tok_hbm, tok.at[me_t])
    lg = local(gain_hbm, gb.at[me_t])
    lw = local(w_hbm, wb)
    pl.semaphore_wait(barrier, len(peers))

    theirs = []
    for xk, far in order:
        j = block(xk, far)
        cp = remote(grad_hbm.at[0, rows((2 * j + 1 - c) * BLK, BLK), :], oth.at[j], core)
        cp.start()
        theirs.append(cp)

    ty = remote(tok_hbm, tok.at[me_t], ypair)
    gy = remote(gain_hbm, gb.at[me_t], ypair)
    ty.start()
    gy.start()
    tz = []
    for k in (1, 3, 2):
        t = remote(tok_hbm, tok.at[me_t], zid(k))
        g = remote(gain_hbm, gb.at[me_t], zid(k))
        t.start()
        g.start()
        tz += [t, g]

    def add_rows(j, r0, extra):
        def body(i, _):
            r = pl.ds(pl.multiple_of(r0 + i * CH, CH), CH)
            v = own[j, r, :].astype(F32)
            for ref, base in extra:
                v = v + ref[pl.ds(pl.multiple_of(base + i * CH, CH), CH), :].astype(F32)
            own[j, r, :] = v.astype(BF16)
            return 0

        lax.fori_loop(0, HALF // CH, body, 0)

    def pair_sum(n):
        xk, far = order[n]
        j = block(xk, far)
        mine[n].wait()
        theirs[n].wait_recv()
        return j

    rs = []

    def xsend(j, half, d, slot):
        cp = remote(own.at[j, pl.ds(half * HALF, HALF), :], xr.at[d, slot], xid(1 if d == 0 else 3))
        cp.start()
        rs.append(cp)
        return cp

    fin = {}
    for far in (True, False):
        n0 = 0 if far else 3
        base = 0 if far else 3
        j2 = pair_sum(n0)
        add_rows(j2, 0, [(oth.at[j2], 0)])
        r0 = xsend(j2, 0, 0, base)
        add_rows(j2, HALF, [(oth.at[j2], HALF)])
        l0 = xsend(j2, 1, 1, base)
        jr = pair_sum(n0 + 1)
        add_rows(jr, HALF, [(oth.at[jr], HALF)])
        r1 = xsend(jr, 1, 0, base + 2)
        jl = pair_sum(n0 + 2)
        add_rows(jl, 0, [(oth.at[jl], 0)])
        l1 = xsend(jl, 0, 1, base + 1)
        r0.wait_recv()
        add_rows(jr, 0, [(oth.at[jr], 0), (xr.at[0, base], 0)])
        r2 = xsend(jr, 0, 0, base + 1)
        l0.wait_recv()
        add_rows(jl, HALF, [(oth.at[jl], HALF), (xr.at[1, base], 0)])
        l2 = xsend(jl, 1, 1, base + 2)
        fin[far] = (r1, r2, l1, l2)

    ty.wait_recv()
    gy.wait_recv()
    for k in (1, 3, 2):
        t = remote(tok.at[pa_t], tok.at[pa_t], zid(k))
        g = remote(gb.at[pa_t], gb.at[pa_t], zid(k))
        t.start()
        g.start()
        tz += [t, g]

    jf = pair_sum(6)
    r1, r2, l1, l2 = fin[True]
    r1.wait_recv()
    l1.wait_recv()
    r2.wait_recv()
    ys = []
    for h, last in ((0, None), (1, l2)):
        if last is not None:
            last.wait_recv()
        add_rows(jf, h * HALF, [(oth.at[jf], h * HALF), (xr.at[0, 1 + h], 0), (xr.at[1, 1 + h], 0)])
        cp = remote(own.at[jf, pl.ds(h * HALF, HALF), :], yr.at[h], yfar)
        cp.start()
        ys.append(cp)

    jo = pair_sum(7)
    for cp in fin[False]:
        cp.wait_recv()
    for cp in ys:
        cp.wait_recv()

    def finish(h, acc):
        def body(i, a):
            r = pl.multiple_of(i * CH, CH)
            rh = pl.ds(pl.multiple_of(h * HALF + i * CH, CH), CH)
            v = own[jo, rh, :].astype(F32) + oth[jo, rh, :].astype(F32)
            v = v + xr[0, 4 + h, pl.ds(r, CH), :].astype(F32)
            v = v + xr[1, 4 + h, pl.ds(r, CH), :].astype(F32)
            v = v + yr[h, pl.ds(r, CH), :].astype(F32)
            gf[rh, :] = v
            s = v * v
            s = s[:8] + s[8:]
            t = s[:, :128]
            for k in range(1, COLS // 128):
                t = t + s[:, k * 128:(k + 1) * 128]
            return a + t

        return lax.fori_loop(0, HALF // CH, body, acc)

    acc = finish(0, jnp.zeros((8, 128), F32))
    acc = finish(1, acc)
    for cp in rs + ys + theirs:
        cp.wait_send()

    slot = 0
    for stage, group in enumerate(([core], [xid(k) for k in (1, 2, 3)], [yid(k) for k in (1, 2, 3)], [zid(k) for k in (1, 2, 3)])):
        nsend[stage] = acc
        cps = []
        for p in group:
            cp = remote(nsend.at[stage], nrecv.at[slot], p)
            cp.start()
            cps.append((cp, slot))
            slot += 1
        for cp, s in cps:
            cp.wait_recv()
            acc = acc + nrecv[s]
    squares = jnp.sum(jnp.sum(acc, axis=0, keepdims=True), axis=1, keepdims=True)
    scale = 0.7 * math.sqrt(FF) / jnp.sqrt(squares + 1e-12)

    lw.wait()

    def perturb(h):
        def body(i, _):
            r = pl.ds(pl.multiple_of(h * HALF + i * CH, CH), CH)
            own[jo, r, :] = (wb[r, :].astype(F32) + scale * gf[r, :]).astype(BF16)
            return 0

        lax.fori_loop(0, HALF // CH, body, 0)

    def piece(j, h):
        return own.at[j, pl.ds(h * HALF, HALF), :]

    def hop(j, h, d):
        cp = remote(piece(j, h), piece(j, h), xid(1 if d == 0 else 3))
        cp.start()
        return cp

    d2d = {}

    def across(xk, far, h):
        j = block(xk, far)
        cp = remote(piece(j, h), oth.at[j, pl.ds(h * HALF, HALF), :], core)
        cp.start()
        d2d[xk, far, h] = cp

    jl, jr, j2 = block(3, False), block(1, False), block(2, False)
    jfl, jfr, jf2 = block(3, True), block(1, True), block(2, True)
    perturb(0)
    cr0 = hop(jo, 0, 0)
    yo0 = remote(piece(jo, 0), piece(jo, 0), yfar)
    yo0.start()
    perturb(1)
    cl1 = hop(jo, 1, 1)
    yo1 = remote(piece(jo, 1), piece(jo, 1), yfar)
    yo1.start()
    cr1 = hop(jo, 1, 0)
    cl0 = hop(jo, 0, 1)
    across(0, False, 0)
    across(0, False, 1)
    lp = local(own.at[jo], pert_hbm)

    lt.wait()
    lg.wait()
    for cp in tz:
        cp.wait_recv()

    def norm_rows(i, _):
        r = pl.ds(pl.multiple_of(i * CH, CH), CH)
        tot = tok[0, r, :].astype(F32)
        for k in range(1, NMP):
            tot = tot + tok[k, r, :].astype(F32)
        mean = jnp.sum(tot, axis=1, keepdims=True) * (1.0 / D)
        dev = None
        for k in range(NMP):
            e = tok[k, r, :].astype(F32) - mean
            dev = e * e if dev is None else dev + e * e
        var = jnp.sum(dev, axis=1, keepdims=True) * (1.0 / D)
        inv = 1.0 / jnp.sqrt(var + 1e-6)
        for k in range(NMP):
            e = (tok[k, r, :].astype(F32) - mean) * inv * gb[k, 0:1, :]
            tok[k, r, :] = e.astype(BF16)
        return 0

    for cp in tz:
        cp.wait_send()
    lax.fori_loop(0, TOK // CH, norm_rows, 0)

    cr0.wait_recv()
    fr = hop(jl, 0, 0)
    across(3, False, 0)
    cl1.wait_recv()
    fl = hop(jr, 1, 1)
    across(1, False, 1)
    yo0.wait_recv()
    yo1.wait_recv()
    fr0, fl1 = hop(jf, 0, 0), hop(jf, 1, 1)
    fr1, fl0 = hop(jf, 1, 0), hop(jf, 0, 1)
    across(0, True, 0)
    across(0, True, 1)
    cr1.wait_recv()
    across(3, False, 1)
    cl0.wait_recv()
    across(1, False, 0)

    NT = 256

    def dots(xk, far, n):
        j = block(xk, far)
        cols = pl.ds(pl.multiple_of(n * NT, NT), NT)
        a0 = tok[j, :, pl.ds(pl.multiple_of(c * BLK, BLK), BLK)]
        a1 = tok[j, :, pl.ds(pl.multiple_of((1 - c) * BLK, BLK), BLK)]
        return jnp.dot(a0, own[j, :, cols], preferred_element_type=F32) + jnp.dot(
            a1, oth[j, :, cols], preferred_element_type=F32
        )

    def multiply(xk, far, first=False):
        d2d[xk, far, 0].wait_recv()
        d2d[xk, far, 1].wait_recv()

        def body(n, _):
            cols = pl.ds(pl.multiple_of(n * NT, NT), NT)
            if first:
                pre[:, cols] = dots(xk, far, n)
            else:
                pre[:, cols] = pre[:, cols] + dots(xk, far, n)
            return 0

        lax.fori_loop(0, COLS // NT, body, 0)

    multiply(0, False, True)
    multiply(0, True)
    multiply(3, False)
    multiply(1, False)
    fr.wait_recv()
    across(2, False, 0)
    fl.wait_recv()
    across(2, False, 1)
    fr0.wait_recv()
    ffr = hop(jfl, 0, 0)
    across(3, True, 0)
    fl1.wait_recv()
    ffl = hop(jfr, 1, 1)
    across(1, True, 1)
    multiply(2, False)
    fr1.wait_recv()
    across(3, True, 1)
    fl0.wait_recv()
    across(1, True, 0)
    multiply(3, True)
    multiply(1, True)
    ffr.wait_recv()
    across(2, True, 0)
    ffl.wait_recv()
    across(2, True, 1)
    d2d[2, True, 0].wait_recv()
    d2d[2, True, 1].wait_recv()

    def last(n, _):
        cols = pl.ds(pl.multiple_of(n * NT, NT), NT)
        v = pre[:, cols] + dots(2, True, n)
        hid[:, cols] = (v * 0.5 * (1.0 + lax.erf(v * (1.0 / math.sqrt(2.0))))).astype(BF16)
        return 0

    lax.fori_loop(0, COLS // NT, last, 0)
    lh = local(hid, hid_hbm)
    done = {id(cp) for cp in rs + ys + theirs + tz}
    for cp in sends:
        if id(cp) not in done:
            cp.wait_send()
    lp.wait()
    lh.wait()


NSEM = 84


def per_device(tokens, ln_gain, weights, grad_partials):
    gain = jnp.broadcast_to(ln_gain.astype(F32)[None, :], (8, FEAT))
    anyspace = pl.BlockSpec(memory_space=pl.ANY)
    return pl.pallas_call(
        kernel,
        out_shape=(
            jax.ShapeDtypeStruct((TOK, COLS), BF16),
            jax.ShapeDtypeStruct((BLK, COLS), BF16),
        ),
        in_specs=[anyspace] * 4,
        out_specs=(anyspace, anyspace),
        scratch_shapes=[
            pltpu.VMEM((8, BLK, COLS), BF16),
            pltpu.VMEM((8, BLK, COLS), BF16),
            pltpu.VMEM((2, 6, HALF, COLS), BF16),
            pltpu.VMEM((2, HALF, COLS), BF16),
            pltpu.VMEM((NMP, TOK, FEAT), BF16),
            pltpu.VMEM((NMP, 8, FEAT), F32),
            pltpu.VMEM((BLK, COLS), F32),
            pltpu.VMEM((BLK, COLS), BF16),
            pltpu.VMEM((TOK, COLS), F32),
            pltpu.VMEM((TOK, COLS), BF16),
            pltpu.VMEM((4, 8, 128), F32),
            pltpu.VMEM((10, 8, 128), F32),
            pltpu.SemaphoreType.DMA((NSEM,)),
            pltpu.SemaphoreType.DMA((NSEM,)),
            pltpu.SemaphoreType.DMA((16,)),
        ],
        compiler_params=pltpu.CompilerParams(
            collective_id=0, has_side_effects=True, vmem_limit_bytes=60 * 1024 * 1024
        ),
    )(tokens, gain, weights, grad_partials)


def solution(mesh):
    torus = Mesh(mesh.devices.reshape(4, 2, 2, 2, 4), AXES)
    placed = (P(DP, MP), P(MP), P(DP, MP), P(DP, None, MP))
    return jax.shard_map(
        per_device, mesh=torus, in_specs=placed, out_specs=(P(DP, MP), P(DP, MP)), check_vma=False
    )
```

time: 412 us -> 213 us (0.52)
  waiting for transfers between devices: 291 us -> 0 us
  Pallas kernels: 0 us -> 206 us
  blocking collectives: 57 us -> 0 us
  matrix products: 33.5 us -> 0 us
  between operations: 16.2 us -> 0.65 us
  other arithmetic: 13 us -> 0 us
  local copies, waits for them, and re-layouts: 1.4 us -> 5.63 us
    pallas_call x0 -> x1, Pallas kernels: none -> 206 us  [per_device(): pl.pallas_call(kernel, out_shape=(jax.ShapeDtypeStruct((TOK, COLS), BF16)...]
    reduce_scatter x1 -> x0, waiting for transfers between devices: 204 us -> none  [per_device(): lax.psum_scatter(grad_partials, DP, scatter_dimension=1, tiled=True)]
    all_gather x2 -> x0, waiting for transfers between devices: 85.6 us -> none  [the longest x1 85.6 us: per_device(): lax.all_gather(perturbed, DP, axis=0, tiled=True)]
    psum x5 -> x0, blocking collectives: 34.1 us -> none  [over_axes(): return functools.reduce(lax.psum, axes, shard)]
    dot_general x1 -> x0, matrix products: 33.5 us -> none  [per_device(): jnp.dot(normed, lax.all_gather(perturbed, DP, axis=0, tiled=True), prefer...]
    all_gather x1 -> x0, blocking collectives: 22.9 us -> none  [per_device(): lax.all_gather(ln_gain, MP, axis=0, tiled=True)]
    reduce_sum x3 -> x0, other arithmetic: 10.3 us -> none  [the longest x1 5.21 us: per_device(): center = jnp.mean(values, axis=1, keepdims=True)]
  transfers between devices with their start and end apart: 3 -> 0, of which waited for: 2 -> 0; matrix products, arithmetic and copies ran while one was open for 3% -> 0% of each run, Pallas kernels for 0% -> 0%
where the time goes in v1:
time: 213 us
  Pallas kernels  206 us (97%)
  local copies, waits for them, and re-layouts  5.63 us (3%)
    pallas_call x1, Pallas kernels, per_device(): pl.pallas_call(kernel, out_shape=(jax.ShapeDtypeStruct((TOK, COLS), BF16)...  206 us
    unnamed x4, local copies, waits for them, and re-layouts  4.33 us

profile of v1, /device:TPU:1, one launch (start us, length us, event | category | flops | bytes accessed | tf_op | source)
XLA Modules:
  0.0 212.7 jit_solution(14939969324885461785)
XLA Ops:
  0.6 1.3 broadcast_in_dim.2.gain_hbm
  1.9 206.4 %shard_map.59 = (bf16[768,1536]{1,0:T(8,128)(2,1)}, bf16[384,1536]{1,0:T(8,128)(2,1)}) custom-call(bf16[768,768]{1,0:T(8,128)(2,1)} %tok_hbm.1, f32[8,768]{1,0:T(8,128)} %broadcast_in_dim.2.gain_hbm, bf16[384,1536]{1,0:T(8,128)(2,1)} %w_hbm.1, bf16[1,6144,1536]{2,1,0:T(8,128)(2,1)} %grad_hbm.1), custom_call_target="tpu_custom_call" | custom-call | tf_op jit(solution)/shard_map/pallas_call | solution.py:390
  208.3 0.0 copy-start
  208.3 3.3 %copy.8 = bf16[768,1536]{1,0:T(8,128)(2,1)} copy(bf16[768,1536]{1,0:T(8,128)(2,1)} %get-tuple-element.4) | data formatting | bytes 4718592
  211.6 0.0 copy-done
  211.6 1.0 copy.9
Async XLA Ops:
  208.3 3.3 %copy-start = (bf16[384,1536]{1,0:T(8,128)(2,1)S(1)}, bf16[384,1536]{1,0:T(8,128)(2,1)}, u32[]{:S(2)}) copy-start(bf16[384,1536]{1,0:T(8,128)(2,1)} %get-tuple-element.5) | copy-start | bytes 3538948

commit v2 on v0

v2 whole, which is shorter than its diff:
```python
import functools
import math

import jax
import jax.numpy as jnp
from jax import lax
from jax.experimental import pallas as pl
from jax.experimental.pallas import tpu as pltpu
from jax.sharding import Mesh
from jax.sharding import PartitionSpec as P

FF = 12288
MP = ("mp_0", "mp_1")
DP = ("dp_0", "dp_1", "dp_2")
AXES = ("dp_0", "dp_1", "dp_2", "mp_0", "mp_1")
MESH = pl.DeviceIdType.MESH

BLK = 384
COLS = 1536
TOK = 768
FEAT = 768
NMP = 8
D = FEAT * NMP
SA = 288
SB = BLK - SA
GA = 224
GB = BLK - GA
CH = 16
NT = 256
NSEM = 128
F32 = jnp.float32
BF16 = jnp.bfloat16
R, L = 0, 1


def kernel(
    tok_hbm, gain_hbm, w_hbm, grad_hbm, hid, pert,
    pb, xa, xb, ya, yb, tok, gb, gf, wb, pre, nsend, nrecv,
    ssem, rsem, lsem,
):
    x, yh, c, yl, z = [lax.axis_index(a) for a in AXES]
    y = yh * 2 + yl

    def xid(k):
        return {"dp_0": lax.rem(x + k, 4)}

    def yid(k):
        yy = lax.rem(y + k, 4)
        return {"dp_1": yy // 2, "mp_0": lax.rem(yy, 2)}

    def zid(k):
        return {"mp_1": lax.rem(z + k, 4)}

    core = {"dp_2": 1 - c}
    ypair = {"mp_0": 1 - yl}
    yfar = {"dp_1": 1 - yh}
    xdev = (xid(1), xid(3))

    count = {"s": 0, "l": 0}
    open_sends = []

    def send(src, dst, dev):
        i = count["s"]
        count["s"] += 1
        cp = pltpu.make_async_remote_copy(
            src_ref=src, dst_ref=dst, send_sem=ssem.at[i], recv_sem=rsem.at[i],
            device_id=dev, device_id_type=MESH,
        )
        cp.start()
        open_sends.append(cp)
        return cp

    def local(src, dst):
        i = count["l"]
        count["l"] += 1
        cp = pltpu.make_async_copy(src, dst, lsem.at[i])
        cp.start()
        return cp

    def rows(start, n):
        return pl.ds(pl.multiple_of(start, 16), n)

    mine0 = c * BLK
    peer0 = (1 - c) * BLK
    peer_dst = c * BLK

    def block(xk, far):
        return lax.rem(x + xk, 4) * 2 + ((1 - yh) if far else yh)

    def own(j, r0, n):
        return pb.at[j, rows(mine0 + r0, n), :]

    barrier = pltpu.get_barrier_semaphore()
    chips = [core, *(xid(k) for k in (1, 2, 3)), *({**xid(k), **core} for k in (1, 2, 3))]
    planes = [{**yid(i), **zid(k)} for i in range(4) for k in range(4) if i or k]
    peers = chips + planes
    for p in peers:
        pl.semaphore_signal(barrier, inc=1, device_id=p, device_id_type=MESH)
    order = [(2, True), (1, True), (3, True), (0, True), (2, False), (1, False), (3, False), (0, False)]
    mine = {}
    for key in order:
        j = block(*key)
        mine[key] = local(grad_hbm.at[0, rows(2 * j * BLK + mine0, BLK), :], own(j, 0, BLK))
    me_t, pa_t = yl * 4 + z, (1 - yl) * 4 + z
    lt = local(tok_hbm, tok.at[me_t])
    lg = local(gain_hbm, gb.at[me_t])
    lw = local(w_hbm, wb)
    pl.semaphore_wait(barrier, len(peers))

    theirs = {}
    HA, HB = SA // 2, SB // 2
    for key in order:
        j = block(*key)
        cuts = (0, HA, SA, BLK) if key == order[0] else (0, BLK)
        theirs[key] = [
            send(grad_hbm.at[0, rows(2 * j * BLK + peer0 + lo, hi - lo), :], pb.at[j, rows(peer_dst + lo, hi - lo), :], core)
            for lo, hi in zip(cuts, cuts[1:])
        ]
    ty = send(tok_hbm, tok.at[me_t], ypair)
    t1 = [send(tok_hbm, tok.at[me_t], zid(k)) for k in (1, 3)]
    gy = send(gain_hbm, gb.at[me_t], ypair)
    g1 = [send(gain_hbm, gb.at[me_t], zid(k)) for k in (1, 2, 3)]

    def add(j, r0, n, extra=()):
        def body(i, _):
            r = rows(mine0 + r0 + i * CH, CH)
            v = pb[j, r, :].astype(F32) + pb[j, rows(peer0 + r0 + i * CH, CH), :].astype(F32)
            for ref, base in extra:
                v = v + ref[rows(base + i * CH, CH), :].astype(F32)
            pb[j, r, :] = v.astype(BF16)
            return 0

        lax.fori_loop(0, n // CH, body, 0)

    def ready(key, first=0):
        if not first:
            mine[key].wait()
        theirs[key][first].wait_recv()
        return block(*key)

    def a_send(j, near, half, d, slot):
        return send(own(j, half * HA, HA), xa.at[d, near, slot], xdev[d])

    def b_send(j, half, d, slot):
        return send(own(j, SA + half * HB, HB), xb.at[d, slot], xdev[d])

    rs = []

    def y_send(key):
        j = block(*key)
        xx = lax.rem(x + key[0], 4)
        add(j, SA, SB)
        cp = send(own(j, SA, SB), yb.at[xx], yfar)
        rs.append(cp)
        return cp

    def a_open(far):
        near = 0 if far else 1
        j = ready((2, far))
        add(j, 0, HA)
        r0 = a_send(j, near, 0, R, 0)
        if far:
            ready((2, far), 1)
        add(j, HA, HA)
        l0 = a_send(j, near, 1, L, 0)
        j = ready((1, far))
        add(j, HA, HA)
        r1 = a_send(j, near, 1, R, 2)
        j = ready((3, far))
        add(j, 0, HA)
        l1 = a_send(j, near, 0, L, 1)
        rs.extend((r0, l0, r1, l1))
        return r0, l0, r1, l1

    def a_pass(far, opened):
        near = 0 if far else 1
        r0, l0, r1, l1 = opened
        jr, jl = block(1, far), block(3, far)
        r0.wait_recv()
        add(jr, 0, HA, [(xa.at[R, near, 0], 0)])
        r2 = a_send(jr, near, 0, R, 1)
        l0.wait_recv()
        add(jl, HA, HA, [(xa.at[L, near, 0], 0)])
        l2 = a_send(jl, near, 1, L, 2)
        rs.extend((r2, l2))
        return r1, r2, l1, l2

    far_a = a_open(True)
    yrb = {}
    ready((2, True), 2)
    for xk in (2, 1, 3):
        yrb[xk] = y_send((xk, True))
    ready((0, True))
    yrb[0] = y_send((0, True))
    far_a = a_pass(True, far_a)
    near_a = a_open(False)

    for cp in t1:
        cp.wait_recv()
    TH = TOK // 2
    left_t, right_t = lax.rem(z + 3, 4), lax.rem(z + 1, 4)

    def pass_tokens(base):
        lo = send(tok.at[base + left_t, pl.ds(0, TH), :], tok.at[base + left_t, pl.ds(0, TH), :], zid(1))
        hi = send(tok.at[base + right_t, pl.ds(TH, TH), :], tok.at[base + right_t, pl.ds(TH, TH), :], zid(3))
        return [lo, hi]

    t2 = pass_tokens(yl * 4)

    jf = block(0, True)
    for cp in far_a:
        cp.wait_recv()
    yra = []
    for h in range(2):
        add(jf, h * HA, HA, [(xa.at[R, 0, 1 + h], 0), (xa.at[L, 0, 1 + h], 0)])
        yra.append(send(own(jf, h * HA, HA), ya.at[h], yfar))
    rs += yra

    ty.wait_recv()
    gy.wait_recv()
    t3 = [send(tok.at[pa_t], tok.at[pa_t], zid(k)) for k in (1, 3)]
    g3 = [send(gb.at[pa_t], gb.at[pa_t], zid(k)) for k in (1, 2, 3)]

    near_a = a_pass(False, near_a)

    def b_add(key, half, extra=()):
        j = block(*key)
        xx = lax.rem(x + key[0], 4)
        add(j, SA + half * HB, HB, [(yb.at[xx], half * HB), *extra])
        return j

    yrb[2].wait_recv()
    br0 = b_send(b_add((2, False), 0), 0, R, 0)
    bl0 = b_send(b_add((2, False), 1), 1, L, 0)
    yrb[1].wait_recv()
    br1 = b_send(b_add((1, False), 1), 1, R, 2)
    yrb[3].wait_recv()
    bl1 = b_send(b_add((3, False), 0), 0, L, 1)
    br0.wait_recv()
    br2 = b_send(b_add((1, False), 0, [(xb.at[R, 0], 0)]), 0, R, 1)
    bl0.wait_recv()
    bl2 = b_send(b_add((3, False), 1, [(xb.at[L, 0], 0)]), 1, L, 2)
    rs += [br0, bl0, br1, bl1, br2, bl2]

    jo = ready((0, False))

    def finish(r0, n, extra, acc):
        def body(i, a):
            rh = rows(r0 + i * CH, CH)
            v = pb[jo, rows(mine0 + r0 + i * CH, CH), :].astype(F32) + pb[jo, rows(peer0 + r0 + i * CH, CH), :].astype(F32)
            for ref, base in extra:
                v = v + ref[rows(base + i * CH, CH), :].astype(F32)
            gf[rh, :] = v
            s = v * v
            s = s[:8] + s[8:]
            t = s[:, :128]
            for k in range(1, COLS // 128):
                t = t + s[:, k * 128:(k + 1) * 128]
            return a + t

        return lax.fori_loop(0, n // CH, body, acc)

    acc = jnp.zeros((8, 128), F32)
    for cp in [*near_a, *yra]:
        cp.wait_recv()
    for h in range(2):
        acc = finish(h * HA, HA, [(xa.at[R, 1, 1 + h], 0), (xa.at[L, 1, 1 + h], 0), (ya.at[h], 0)], acc)
    yrb[0].wait_recv()
    for cp in (br1, bl1, br2, bl2):
        cp.wait_recv()
    for h in range(2):
        acc = finish(SA + h * HB, HB, [(yb.at[x], h * HB), (xb.at[R, 1 + h], 0), (xb.at[L, 1 + h], 0)], acc)
    for cp in rs:
        cp.wait_send()
    done = list(rs)

    slot = 0
    for stage, group in enumerate((chips, planes)):
        nsend[stage] = acc
        cps = []
        for p in group:
            cps.append((send(nsend.at[stage], nrecv.at[slot], p), slot))
            slot += 1
        if stage == 1:
            for cp in t3:
                cp.wait_recv()
            t4 = pass_tokens((1 - yl) * 4)
        for cp, s in cps:
            cp.wait_recv()
            acc = acc + nrecv[s]
    squares = jnp.sum(jnp.sum(acc, axis=0, keepdims=True), axis=1, keepdims=True)
    scale = 0.7 * math.sqrt(FF) / jnp.sqrt(squares + 1e-12)

    lw.wait()

    def perturb(i, _):
        r = rows(i * CH, CH)
        v = (wb[r, :].astype(F32) + scale * gf[r, :]).astype(BF16)
        pb[jo, rows(mine0 + i * CH, CH), :] = v
        pert[r, :] = v
        return 0

    PA, PB = GA // 2, GB // 2

    def go(j, r0, n, dev):
        return send(own(j, r0, n), own(j, r0, n), dev)

    d2d = {}

    def across(xk, far, r0, n):
        j = block(xk, far)
        d2d.setdefault((xk, far), []).append(go(j, r0, n, core))

    lax.fori_loop(GA // CH, BLK // CH, perturb, 0)
    ob = [go(jo, GA, GB, xdev[d]) for d in (R, L)]
    lax.fori_loop(0, GA // CH, perturb, 0)
    ya1 = go(jo, 0, GA, yfar)
    oa = [go(jo, 0, GA, xdev[d]) for d in (R, L)]
    across(0, False, 0, BLK)
    yb1 = go(jo, GA, GB, yfar)

    ob[R].wait_recv()
    fb = [go(block(3, False), GA, PB, xdev[R])]
    yl_b = go(block(3, False), GA, GB, yfar)
    across(3, False, GA, GB)
    ob[L].wait_recv()
    fb.append(go(block(1, False), GA + PB, PB, xdev[L]))
    yr_b = go(block(1, False), GA, GB, yfar)
    across(1, False, GA, GB)
    ya1.wait_recv()
    across(0, True, 0, GA)

    lt.wait()
    lg.wait()
    for cp in [*t2, *t4, *g1, *g3]:
        cp.wait_recv()
    tsent = [*t2, *t3, *t4]
    for cp in tsent:
        cp.wait_send()
    done += tsent

    def norm_rows(i, _):
        r = rows(i * CH, CH)
        tot = tok[0, r, :].astype(F32)
        for k in range(1, NMP):
            tot = tot + tok[k, r, :].astype(F32)
        mean = jnp.sum(tot, axis=1, keepdims=True) * (1.0 / D)
        dev = None
        for k in range(NMP):
            e = tok[k, r, :].astype(F32) - mean
            dev = e * e if dev is None else dev + e * e
        var = jnp.sum(dev, axis=1, keepdims=True) * (1.0 / D)
        inv = 1.0 / jnp.sqrt(var + 1e-6)
        for k in range(NMP):
            e = (tok[k, r, :].astype(F32) - mean) * inv * gb[k].astype(F32)
            tok[k, r, :] = e.astype(BF16)
        return 0

    lax.fori_loop(0, TOK // CH, norm_rows, 0)

    def dots(j, n):
        cols = pl.ds(pl.multiple_of(n * NT, NT), NT)
        return jnp.dot(tok[j], pb[j, :, cols], preferred_element_type=F32)

    def multiply(xk, far, first=False):
        j = block(xk, far)
        for cp in d2d[xk, far]:
            cp.wait_recv()

        def body(n, _):
            cols = pl.ds(pl.multiple_of(n * NT, NT), NT)
            if first:
                pre[:, cols] = dots(j, n)
            else:
                pre[:, cols] = pre[:, cols] + dots(j, n)
            return 0

        lax.fori_loop(0, COLS // NT, body, 0)

    oa[R].wait_recv()
    fa = [go(block(3, False), 0, PA, xdev[R])]
    across(3, False, 0, GA)
    oa[L].wait_recv()
    fa.append(go(block(1, False), PA, PA, xdev[L]))
    across(1, False, 0, GA)
    fra = [go(block(0, True), d * PA, PA, xdev[d]) for d in (R, L)]
    frb = [go(block(0, True), (1 - d) * PA, PA, xdev[d]) for d in (R, L)]
    yb1.wait_recv()
    across(0, True, GA, GB)
    fb[R].wait_recv()
    y2 = [go(block(2, False), GA, PB, yfar)]
    across(2, False, GA, PB)
    fb[L].wait_recv()
    y2.append(go(block(2, False), GA + PB, PB, yfar))
    across(2, False, GA + PB, PB)
    multiply(0, False, True)
    multiply(0, True)
    multiply(3, False)
    fa[R].wait_recv()
    across(2, False, 0, PA)
    fa[L].wait_recv()
    across(2, False, PA, PA)
    multiply(1, False)
    yl_b.wait_recv()
    across(3, True, GA, GB)
    yr_b.wait_recv()
    across(1, True, GA, GB)
    fra[R].wait_recv()
    ffa = [go(block(3, True), 0, PA, xdev[R])]
    across(3, True, 0, PA)
    fra[L].wait_recv()
    ffa.append(go(block(1, True), PA, PA, xdev[L]))
    across(1, True, PA, PA)
    multiply(2, False)
    frb[R].wait_recv()
    across(3, True, PA, PA)
    frb[L].wait_recv()
    across(1, True, 0, PA)
    for k in range(2):
        y2[k].wait_recv()
        across(2, True, GA + k * PB, PB)
    multiply(3, True)
    multiply(1, True)
    for k in range(2):
        ffa[k].wait_recv()
        across(2, True, k * PA, PA)
    for cp in d2d[2, True]:
        cp.wait_recv()
    jl = block(2, True)

    def last(n, _):
        cols = pl.ds(pl.multiple_of(n * NT, NT), NT)
        v = pre[:, cols] + dots(jl, n)
        hid[:, cols] = (v * 0.5 * (1.0 + lax.erf(v * (1.0 / math.sqrt(2.0))))).astype(BF16)
        return 0

    lax.fori_loop(0, COLS // NT, last, 0)
    closed = {id(cp) for cp in done}
    for cp in open_sends:
        if id(cp) not in closed:
            cp.wait_send()


def per_device(tokens, ln_gain, weights, grad_partials):
    gain = ln_gain.reshape(1, FEAT)
    hbm = pl.BlockSpec(memory_space=pltpu.HBM)
    return pl.pallas_call(
        kernel,
        out_shape=(
            pltpu.VMEM((TOK, COLS), BF16),
            pltpu.VMEM((BLK, COLS), BF16),
        ),
        in_specs=[hbm] * 4,
        out_specs=(pl.BlockSpec(memory_space=pltpu.VMEM),) * 2,
        scratch_shapes=[
            pltpu.VMEM((8, 2 * BLK, COLS), BF16),
            pltpu.VMEM((2, 2, 3, SA // 2, COLS), BF16),
            pltpu.VMEM((2, 3, SB // 2, COLS), BF16),
            pltpu.VMEM((2, SA // 2, COLS), BF16),
            pltpu.VMEM((4, SB, COLS), BF16),
            pltpu.VMEM((NMP, TOK, FEAT), BF16),
            pltpu.VMEM((NMP, 1, FEAT), BF16),
            pltpu.VMEM((BLK, COLS), F32),
            pltpu.VMEM((BLK, COLS), BF16),
            pltpu.VMEM((TOK, COLS), F32),
            pltpu.VMEM((2, 8, 128), F32),
            pltpu.VMEM((22, 8, 128), F32),
            pltpu.SemaphoreType.DMA((NSEM,)),
            pltpu.SemaphoreType.DMA((NSEM,)),
            pltpu.SemaphoreType.DMA((16,)),
        ],
        compiler_params=pltpu.CompilerParams(
            collective_id=0, has_side_effects=True, vmem_limit_bytes=50 * 1024 * 1024
        ),
    )(tokens, gain, weights, grad_partials)


def solution(mesh):
    torus = Mesh(mesh.devices.reshape(4, 2, 2, 2, 4), AXES)
    placed = (P(DP, MP), P(MP), P(DP, MP), P(DP, None, MP))
    return jax.shard_map(
        per_device, mesh=torus, in_specs=placed, out_specs=(P(DP, MP), P(DP, MP)), check_vma=False
    )
```

time: 412 us -> 166 us (0.40)
  waiting for transfers between devices: 291 us -> 0 us
  Pallas kernels: 0 us -> 163 us
  blocking collectives: 57 us -> 0 us
  matrix products: 33.5 us -> 0 us
  between operations: 16.2 us -> 0.64 us
  other arithmetic: 13 us -> 0 us
    reduce_scatter x1 -> x0, waiting for transfers between devices: 204 us -> none  [per_device(): lax.psum_scatter(grad_partials, DP, scatter_dimension=1, tiled=True)]
    pallas_call x0 -> x1, Pallas kernels: none -> 163 us  [per_device(): pl.pallas_call(kernel, out_shape=(pltpu.VMEM((TOK, COLS), BF16), pltpu.VM...]
    all_gather x2 -> x0, waiting for transfers between devices: 85.6 us -> none  [the longest x1 85.6 us: per_device(): lax.all_gather(perturbed, DP, axis=0, tiled=True)]
    psum x5 -> x0, blocking collectives: 34.1 us -> none  [over_axes(): return functools.reduce(lax.psum, axes, shard)]
    dot_general x1 -> x0, matrix products: 33.5 us -> none  [per_device(): jnp.dot(normed, lax.all_gather(perturbed, DP, axis=0, tiled=True), prefer...]
    all_gather x1 -> x0, blocking collectives: 22.9 us -> none  [per_device(): lax.all_gather(ln_gain, MP, axis=0, tiled=True)]
    reduce_sum x3 -> x0, other arithmetic: 10.3 us -> none  [the longest x1 5.21 us: per_device(): center = jnp.mean(values, axis=1, keepdims=True)]
  transfers between devices with their start and end apart: 3 -> 0, of which waited for: 2 -> 0; matrix products, arithmetic and copies ran while one was open for 3% -> 0% of each run, Pallas kernels for 0% -> 0%
where the time goes in v2:
time: 166 us
  Pallas kernels  163 us (98%)
  local copies, waits for them, and re-layouts  3.11 us (2%)
    pallas_call x1, Pallas kernels, per_device(): pl.pallas_call(kernel, out_shape=(pltpu.VMEM((TOK, COLS), BF16), pltpu.VM...  163 us

profile of v2, /device:TPU:1, one launch (start us, length us, event | category | flops | bytes accessed | tf_op | source)
XLA Modules:
  0.0 166.3 jit_solution(8464840146723957876)
XLA Ops:
  0.6 0.7 reshape.7.gain_hbm
  1.3 162.6 %shard_map.59 = (bf16[768,1536]{1,0:T(8,128)(2,1)S(1)}, bf16[384,1536]{1,0:T(8,128)(2,1)S(1)}) custom-call(bf16[768,768]{1,0:T(8,128)(2,1)} %tok_hbm.1, bf16[1,768]{1,0:T(2,128)(2,1)S(1)} %reshape.7.gain_hbm, bf16[384,1536]{1,0:T(8,128)(2,1)} %w_hbm.1, bf16[1,6144,1536]{2,1,0:T(8,128)(2,1)} %grad_hbm.1), custom_call_target="tpu_custom_call" | custom-call | tf_op jit(solution)/shard_map/pallas_call | solution.py:447
  163.9 1.4 copy.8
  165.3 1.0 copy.9

commit v3 on v2

--- a/solution.py
+++ b/solution.py
@@ -302,14 +302,15 @@
 
     PA, PB = GA // 2, GB // 2
 
-    def go(j, r0, n, dev):
-        return send(own(j, r0, n), own(j, r0, n), dev)
+    def go(j, r0, n, dev, c0=0, cn=COLS):
+        ref = pb.at[j, rows(mine0 + r0, n), pl.ds(c0, cn)]
+        return send(ref, ref, dev)
 
     d2d = {}
 
-    def across(xk, far, r0, n):
+    def across(xk, far, r0, n, part=0, c0=0, cn=COLS):
         j = block(xk, far)
-        d2d.setdefault((xk, far), []).append(go(j, r0, n, core))
+        d2d.setdefault((xk, far, part), []).append(go(j, r0, n, core, c0, cn))
 
     lax.fori_loop(GA // CH, BLK // CH, perturb, 0)
     ob = [go(jo, GA, GB, xdev[d]) for d in (R, L)]
@@ -364,7 +365,7 @@
 
     def multiply(xk, far, first=False):
         j = block(xk, far)
-        for cp in d2d[xk, far]:
+        for cp in d2d[xk, far, 0]:
             cp.wait_recv()
 
         def body(n, _):
@@ -405,27 +406,29 @@
     across(3, True, GA, GB)
     yr_b.wait_recv()
     across(1, True, GA, GB)
+    CN = COLS // 2
     fra[R].wait_recv()
-    ffa = [go(block(3, True), 0, PA, xdev[R])]
+    ffa = [[go(block(3, True), 0, PA, xdev[R], q * CN, CN) for q in range(2)]]
     across(3, True, 0, PA)
     fra[L].wait_recv()
-    ffa.append(go(block(1, True), PA, PA, xdev[L]))
+    ffa.append([go(block(1, True), PA, PA, xdev[L], q * CN, CN) for q in range(2)])
     across(1, True, PA, PA)
     multiply(2, False)
     frb[R].wait_recv()
     across(3, True, PA, PA)
     frb[L].wait_recv()
     across(1, True, 0, PA)
+    multiply(3, True)
     for k in range(2):
         y2[k].wait_recv()
         across(2, True, GA + k * PB, PB)
-    multiply(3, True)
+    for k in range(2):
+        ffa[k][0].wait_recv()
+        across(2, True, k * PA, PA, 0, 0, CN)
     multiply(1, True)
     for k in range(2):
-        ffa[k].wait_recv()
-        across(2, True, k * PA, PA)
-    for cp in d2d[2, True]:
-        cp.wait_recv()
+        ffa[k][1].wait_recv()
+        across(2, True, k * PA, PA, 1, CN, CN)
     jl = block(2, True)
 
     def last(n, _):
@@ -434,7 +437,10 @@
         hid[:, cols] = (v * 0.5 * (1.0 + lax.erf(v * (1.0 / math.sqrt(2.0))))).astype(BF16)
         return 0
 
-    lax.fori_loop(0, COLS // NT, last, 0)
+    for q in range(2):
+        for cp in d2d[2, True, q]:
+            cp.wait_recv()
+        lax.fori_loop(q * CN // NT, (q + 1) * CN // NT, last, 0)
     closed = {id(cp) for cp in done}
     for cp in open_sends:
         if id(cp) not in closed:

time: 166 us -> 163 us (0.982)
  Pallas kernels: 163 us -> 159 us
    pallas_call x1, Pallas kernels: 163 us -> 159 us  [per_device(): pl.pallas_call(kernel, out_shape=(pltpu.VMEM((TOK, COLS), BF16), pltpu.VM...]
where the time goes in v3:
time: 163 us; the launch traced here: 162 us
  Pallas kernels  159 us (98%)
  local copies, waits for them, and re-layouts  3.11 us (2%)
    pallas_call x1, Pallas kernels, per_device(): pl.pallas_call(kernel, out_shape=(pltpu.VMEM((TOK, COLS), BF16), pltpu.VM...  159 us

profile of v3, /device:TPU:1, one launch (start us, length us, event | category | flops | bytes accessed | tf_op | source)
XLA Modules:
  0.0 162.4 jit_solution(5644659775831095989)
XLA Ops:
  0.6 0.7 reshape.7.gain_hbm
  1.3 158.7 %shard_map.59 = (bf16[768,1536]{1,0:T(8,128)(2,1)S(1)}, bf16[384,1536]{1,0:T(8,128)(2,1)S(1)}) custom-call(bf16[768,768]{1,0:T(8,128)(2,1)} %tok_hbm.1, bf16[1,768]{1,0:T(2,128)(2,1)S(1)} %reshape.7.gain_hbm, bf16[384,1536]{1,0:T(8,128)(2,1)} %w_hbm.1, bf16[1,6144,1536]{2,1,0:T(8,128)(2,1)} %grad_hbm.1), custom_call_target="tpu_custom_call" | custom-call | tf_op jit(solution)/shard_map/pallas_call | solution.py:453
  160.0 1.4 copy.8
  161.4 1.0 copy.9

commit v4 on v3

--- a/solution.py
+++ b/solution.py
@@ -27,7 +27,8 @@
 GB = BLK - GA
 CH = 16
 NT = 256
-NSEM = 128
+NSEM = 52
+GPAD = 1024
 F32 = jnp.float32
 BF16 = jnp.bfloat16
 R, L = 0, 1
@@ -58,17 +59,45 @@
 
     count = {"s": 0, "l": 0}
     open_sends = []
-
-    def send(src, dst, dev):
-        i = count["s"]
-        count["s"] += 1
+    closed = set()
+    again = []
+    slot_of = {}
+
+    def send(src, dst, dev, at=None):
+        if at is None:
+            at = again.pop() if again else count["s"]
+            if at == count["s"]:
+                count["s"] += 1
+        i = at
         cp = pltpu.make_async_remote_copy(
             src_ref=src, dst_ref=dst, send_sem=ssem.at[i], recv_sem=rsem.at[i],
             device_id=dev, device_id_type=MESH,
         )
         cp.start()
         open_sends.append(cp)
+        slot_of[id(cp)] = i
         return cp
+
+    def group(src, dsts, devs):
+        at = count["s"]
+        count["s"] += 1
+        for dst, dev in zip(dsts, devs):
+            closed.add(id(send(src, dst, dev, at)))
+        return at
+
+    def group_wait(at, ref):
+        cp = pltpu.make_async_remote_copy(
+            src_ref=ref, dst_ref=ref, send_sem=ssem.at[at], recv_sem=rsem.at[at],
+            device_id=core, device_id_type=MESH,
+        )
+        cp.wait_recv()
+        cp.wait_send()
+
+    def flush(cps):
+        for cp in cps:
+            if id(cp) not in closed:
+                closed.add(id(cp))
+                cp.wait_send()
 
     def local(src, dst):
         i = count["l"]
@@ -102,8 +131,11 @@
         j = block(*key)
         mine[key] = local(grad_hbm.at[0, rows(2 * j * BLK + mine0, BLK), :], own(j, 0, BLK))
     me_t, pa_t = yl * 4 + z, (1 - yl) * 4 + z
+    def gains(k):
+        return gb.at[pl.ds(pl.multiple_of(k * GPAD, GPAD), FEAT)]
+
     lt = local(tok_hbm, tok.at[me_t])
-    lg = local(gain_hbm, gb.at[me_t])
+    lg = local(gain_hbm, gains(me_t))
     lw = local(w_hbm, wb)
     pl.semaphore_wait(barrier, len(peers))
 
@@ -118,8 +150,8 @@
         ]
     ty = send(tok_hbm, tok.at[me_t], ypair)
     t1 = [send(tok_hbm, tok.at[me_t], zid(k)) for k in (1, 3)]
-    gy = send(gain_hbm, gb.at[me_t], ypair)
-    g1 = [send(gain_hbm, gb.at[me_t], zid(k)) for k in (1, 2, 3)]
+    gy = send(gain_hbm, gains(me_t), ypair)
+    g1 = group(gain_hbm, [gains(me_t)] * 3, [zid(k) for k in (1, 2, 3)])
 
     def add(j, r0, n, extra=()):
         def body(i, _):
@@ -219,9 +251,10 @@
     ty.wait_recv()
     gy.wait_recv()
     t3 = [send(tok.at[pa_t], tok.at[pa_t], zid(k)) for k in (1, 3)]
-    g3 = [send(gb.at[pa_t], gb.at[pa_t], zid(k)) for k in (1, 2, 3)]
+    g3 = group(gains(pa_t), [gains(pa_t)] * 3, [zid(k) for k in (1, 2, 3)])
 
     near_a = a_pass(False, near_a)
+    early = list(rs)
 
     def b_add(key, half, extra=()):
         j = block(*key)
@@ -261,6 +294,8 @@
         return lax.fori_loop(0, n // CH, body, acc)
 
     acc = jnp.zeros((8, 128), F32)
+    phase = [*early, *(cp for cps in theirs.values() for cp in cps), ty, gy, *t1]
+    flush(phase)
     for cp in [*near_a, *yra]:
         cp.wait_recv()
     for h in range(2):
@@ -270,26 +305,26 @@
         cp.wait_recv()
     for h in range(2):
         acc = finish(SA + h * HB, HB, [(yb.at[x], h * HB), (xb.at[R, 1 + h], 0), (xb.at[L, 1 + h], 0)], acc)
-    for cp in rs:
-        cp.wait_send()
-    done = list(rs)
+    flush(rs)
+    phase += [cp for cp in rs if id(cp) not in {id(e) for e in early}]
 
     slot = 0
-    for stage, group in enumerate((chips, planes)):
+    for stage, devs in enumerate((chips, planes)):
         nsend[stage] = acc
-        cps = []
-        for p in group:
-            cps.append((send(nsend.at[stage], nrecv.at[slot], p), slot))
-            slot += 1
+        n = len(devs)
+        at = group(nsend.at[stage], [nrecv.at[slot + k] for k in range(n)], devs)
         if stage == 1:
             for cp in t3:
                 cp.wait_recv()
             t4 = pass_tokens((1 - yl) * 4)
-        for cp, s in cps:
-            cp.wait_recv()
-            acc = acc + nrecv[s]
+        group_wait(at, nrecv.at[pl.ds(slot, n)])
+        for k in range(n):
+            acc = acc + nrecv[slot + k]
+        slot += n
     squares = jnp.sum(jnp.sum(acc, axis=0, keepdims=True), axis=1, keepdims=True)
     scale = 0.7 * math.sqrt(FF) / jnp.sqrt(squares + 1e-12)
+
+    again += sorted((slot_of[id(cp)] for cp in phase), reverse=True)
 
     lw.wait()
 
@@ -320,25 +355,26 @@
     across(0, False, 0, BLK)
     yb1 = go(jo, GA, GB, yfar)
 
+    old = list(open_sends)
+
     ob[R].wait_recv()
-    fb = [go(block(3, False), GA, PB, xdev[R])]
     yl_b = go(block(3, False), GA, GB, yfar)
     across(3, False, GA, GB)
     ob[L].wait_recv()
-    fb.append(go(block(1, False), GA + PB, PB, xdev[L]))
     yr_b = go(block(1, False), GA, GB, yfar)
     across(1, False, GA, GB)
     ya1.wait_recv()
+    fra = [go(block(0, True), 0, GA, xdev[d]) for d in (R, L)]
+    fb = [go(block(3, False), GA, PB, xdev[R]), go(block(1, False), GA + PB, PB, xdev[L])]
     across(0, True, 0, GA)
 
     lt.wait()
     lg.wait()
-    for cp in [*t2, *t4, *g1, *g3]:
-        cp.wait_recv()
-    tsent = [*t2, *t3, *t4]
-    for cp in tsent:
-        cp.wait_send()
-    done += tsent
+    for cp in [*t2, *t4]:
+        cp.wait_recv()
+    for at in (g1, g3):
+        group_wait(at, gb.at[pl.ds(0, 3 * FEAT)])
+    flush([*t2, *t3, *t4])
 
     def norm_rows(i, _):
         r = rows(i * CH, CH)
@@ -353,7 +389,7 @@
         var = jnp.sum(dev, axis=1, keepdims=True) * (1.0 / D)
         inv = 1.0 / jnp.sqrt(var + 1e-6)
         for k in range(NMP):
-            e = (tok[k, r, :].astype(F32) - mean) * inv * gb[k].astype(F32)
+            e = (tok[k, r, :].astype(F32) - mean) * inv * gb[pl.ds(k * GPAD, FEAT)].astype(F32).reshape(1, FEAT)
             tok[k, r, :] = e.astype(BF16)
         return 0
 
@@ -363,10 +399,11 @@
         cols = pl.ds(pl.multiple_of(n * NT, NT), NT)
         return jnp.dot(tok[j], pb[j, :, cols], preferred_element_type=F32)
 
-    def multiply(xk, far, first=False):
+    def multiply(xk, far, first=False, lo=0, hi=COLS):
         j = block(xk, far)
-        for cp in d2d[xk, far, 0]:
-            cp.wait_recv()
+        if lo == 0:
+            for cp in d2d[xk, far, 0]:
+                cp.wait_recv()
 
         def body(n, _):
             cols = pl.ds(pl.multiple_of(n * NT, NT), NT)
@@ -376,7 +413,7 @@
                 pre[:, cols] = pre[:, cols] + dots(j, n)
             return 0
 
-        lax.fori_loop(0, COLS // NT, body, 0)
+        lax.fori_loop(lo // NT, hi // NT, body, 0, unroll=3)
 
     oa[R].wait_recv()
     fa = [go(block(3, False), 0, PA, xdev[R])]
@@ -384,51 +421,45 @@
     oa[L].wait_recv()
     fa.append(go(block(1, False), PA, PA, xdev[L]))
     across(1, False, 0, GA)
-    fra = [go(block(0, True), d * PA, PA, xdev[d]) for d in (R, L)]
-    frb = [go(block(0, True), (1 - d) * PA, PA, xdev[d]) for d in (R, L)]
     yb1.wait_recv()
     across(0, True, GA, GB)
-    fb[R].wait_recv()
-    y2 = [go(block(2, False), GA, PB, yfar)]
-    across(2, False, GA, PB)
-    fb[L].wait_recv()
-    y2.append(go(block(2, False), GA + PB, PB, yfar))
-    across(2, False, GA + PB, PB)
     multiply(0, False, True)
     multiply(0, True)
     multiply(3, False)
-    fa[R].wait_recv()
-    across(2, False, 0, PA)
-    fa[L].wait_recv()
-    across(2, False, PA, PA)
     multiply(1, False)
+    flush(old)
+    CN = 2 * COLS // 3
+    cuts = ((0, CN), (CN, COLS - CN))
+    fra[R].wait_recv()
+    ffa = [[go(block(3, True), 0, PA, xdev[R], *q) for q in cuts]]
+    across(3, True, 0, GA)
+    fra[L].wait_recv()
+    ffa.append([go(block(1, True), PA, PA, xdev[L], *q) for q in cuts])
+    across(1, True, 0, GA)
+    y2 = []
+    for k in range(2):
+        fb[k].wait_recv()
+        y2.append(go(block(2, False), GA + k * PB, PB, yfar))
+        across(2, False, GA + k * PB, PB)
     yl_b.wait_recv()
     across(3, True, GA, GB)
     yr_b.wait_recv()
     across(1, True, GA, GB)
-    CN = COLS // 2
-    fra[R].wait_recv()
-    ffa = [[go(block(3, True), 0, PA, xdev[R], q * CN, CN) for q in range(2)]]
-    across(3, True, 0, PA)
-    fra[L].wait_recv()
-    ffa.append([go(block(1, True), PA, PA, xdev[L], q * CN, CN) for q in range(2)])
-    across(1, True, PA, PA)
-    multiply(2, False)
-    frb[R].wait_recv()
-    across(3, True, PA, PA)
-    frb[L].wait_recv()
-    across(1, True, 0, PA)
     multiply(3, True)
+    multiply(1, True)
+    for k in range(2):
+        fa[k].wait_recv()
+        across(2, False, k * PA, PA)
+    older = [*fra, *fb, yl_b, yr_b, *fa, *d2d[3, True, 0], *d2d[1, True, 0], *d2d[2, False, 0]]
+    multiply(2, False, False, 0, COLS // 2)
     for k in range(2):
         y2[k].wait_recv()
         across(2, True, GA + k * PB, PB)
     for k in range(2):
         ffa[k][0].wait_recv()
-        across(2, True, k * PA, PA, 0, 0, CN)
-    multiply(1, True)
-    for k in range(2):
-        ffa[k][1].wait_recv()
-        across(2, True, k * PA, PA, 1, CN, CN)
+        across(2, True, k * PA, PA, 0, *cuts[0])
+    multiply(2, False, False, COLS // 2, COLS)
+    flush(older)
     jl = block(2, True)
 
     def last(n, _):
@@ -437,18 +468,24 @@
         hid[:, cols] = (v * 0.5 * (1.0 + lax.erf(v * (1.0 / math.sqrt(2.0))))).astype(BF16)
         return 0
 
-    for q in range(2):
-        for cp in d2d[2, True, q]:
-            cp.wait_recv()
-        lax.fori_loop(q * CN // NT, (q + 1) * CN // NT, last, 0)
-    closed = {id(cp) for cp in done}
-    for cp in open_sends:
-        if id(cp) not in closed:
-            cp.wait_send()
+    def finish_columns(lo, hi):
+        lax.fori_loop(lo // NT, hi // NT, last, 0, unroll=2)
+
+    for cp in d2d[2, True, 0]:
+        cp.wait_recv()
+    finish_columns(0, CN // 2)
+    for k in range(2):
+        ffa[k][1].wait_recv()
+        across(2, True, k * PA, PA, 1, *cuts[1])
+    finish_columns(CN // 2, CN)
+    for cp in d2d[2, True, 1]:
+        cp.wait_recv()
+    finish_columns(CN, COLS)
+    flush(open_sends)
+    assert count["s"] <= NSEM and count["l"] == 11, count
 
 
 def per_device(tokens, ln_gain, weights, grad_partials):
-    gain = ln_gain.reshape(1, FEAT)
     hbm = pl.BlockSpec(memory_space=pltpu.HBM)
     return pl.pallas_call(
         kernel,
@@ -465,7 +502,7 @@
             pltpu.VMEM((2, SA // 2, COLS), BF16),
             pltpu.VMEM((4, SB, COLS), BF16),
             pltpu.VMEM((NMP, TOK, FEAT), BF16),
-            pltpu.VMEM((NMP, 1, FEAT), BF16),
+            pltpu.VMEM((NMP * GPAD,), BF16),
             pltpu.VMEM((BLK, COLS), F32),
             pltpu.VMEM((BLK, COLS), BF16),
             pltpu.VMEM((TOK, COLS), F32),
@@ -473,12 +510,12 @@
             pltpu.VMEM((22, 8, 128), F32),
             pltpu.SemaphoreType.DMA((NSEM,)),
             pltpu.SemaphoreType.DMA((NSEM,)),
-            pltpu.SemaphoreType.DMA((16,)),
+            pltpu.SemaphoreType.DMA((11,)),
         ],
         compiler_params=pltpu.CompilerParams(
             collective_id=0, has_side_effects=True, vmem_limit_bytes=50 * 1024 * 1024
         ),
-    )(tokens, gain, weights, grad_partials)
+    )(tokens, ln_gain, weights, grad_partials)
 
 
 def solution(mesh):

time: 163 us -> 160 us (0.982)
  Pallas kernels: 159 us -> 156 us
    pallas_call x1, Pallas kernels: 159 us -> 156 us  [per_device(): pl.pallas_call(kernel, out_shape=(pltpu.VMEM((TOK, COLS), BF16), pltpu.VM...]
where the time goes in v4:
time: 160 us
  Pallas kernels  156 us (98%)
  local copies, waits for them, and re-layouts  3.1 us (2%)
    pallas_call x1, Pallas kernels, per_device(): pl.pallas_call(kernel, out_shape=(pltpu.VMEM((TOK, COLS), BF16), pltpu.VM...  156 us

profile of v4, /device:TPU:1, one launch (start us, length us, event | category | flops | bytes accessed | tf_op | source)
XLA Modules:
  0.0 159.7 jit_solution(12146293970742003682)
XLA Ops:
  0.6 0.0 copy-start
  0.6 0.7 copy-done
  1.3 156.0 %shard_map.59 = (bf16[768,1536]{1,0:T(8,128)(2,1)S(1)}, bf16[384,1536]{1,0:T(8,128)(2,1)S(1)}) custom-call(bf16[768,768]{1,0:T(8,128)(2,1)} %tok_hbm.1, bf16[768]{0:T(1024)(128)(2,1)S(1)} %copy-done, bf16[384,1536]{1,0:T(8,128)(2,1)} %w_hbm.1, bf16[1,6144,1536]{2,1,0:T(8,128)(2,1)} %grad_hbm.1), custom_call_target="tpu_custom_call" | custom-call | tf_op jit(solution)/shard_map/pallas_call | solution.py:490
  157.3 1.4 copy.8
  158.7 1.0 copy.9
Async XLA Ops:
  0.6 0.7 copy-start

commit v5 on v4

--- a/solution.py
+++ b/solution.py
@@ -277,34 +277,60 @@
 
     jo = ready((0, False))
 
+    def terms(r0, i, extra):
+        v = pb[jo, rows(mine0 + r0 + i * CH, CH), :].astype(F32)
+        v = v + pb[jo, rows(peer0 + r0 + i * CH, CH), :].astype(F32)
+        for ref, base in extra:
+            v = v + ref[rows(base + i * CH, CH), :].astype(F32)
+        return v
+
+    def squared(v):
+        s = v * v
+        s = s[:8] + s[8:]
+        t = s[:, :128]
+        for k in range(1, COLS // 128):
+            t = t + s[:, k * 128:(k + 1) * 128]
+        return t
+
+    def gather_terms(r0, n, extra):
+        def body(i, _):
+            gf[rows(r0 + i * CH, CH), :] = terms(r0, i, extra)
+            return 0
+
+        lax.fori_loop(0, n // CH, body, 0)
+
     def finish(r0, n, extra, acc):
         def body(i, a):
-            rh = rows(r0 + i * CH, CH)
-            v = pb[jo, rows(mine0 + r0 + i * CH, CH), :].astype(F32) + pb[jo, rows(peer0 + r0 + i * CH, CH), :].astype(F32)
-            for ref, base in extra:
-                v = v + ref[rows(base + i * CH, CH), :].astype(F32)
-            gf[rh, :] = v
-            s = v * v
-            s = s[:8] + s[8:]
-            t = s[:, :128]
-            for k in range(1, COLS // 128):
-                t = t + s[:, k * 128:(k + 1) * 128]
-            return a + t
+            v = terms(r0, i, extra)
+            gf[rows(r0 + i * CH, CH), :] = v
+            return a + squared(v)
+
+        return lax.fori_loop(0, n // CH, body, acc)
+
+    def finish_last(r0, n, ref, acc):
+        def body(i, a):
+            r = rows(r0 + i * CH, CH)
+            v = gf[r, :] + ref[rows(i * CH, CH), :].astype(F32)
+            gf[r, :] = v
+            return a + squared(v)
 
         return lax.fori_loop(0, n // CH, body, acc)
 
     acc = jnp.zeros((8, 128), F32)
     phase = [*early, *(cp for cps in theirs.values() for cp in cps), ty, gy, *t1]
+    for cp in near_a:
+        cp.wait_recv()
+    for h in range(2):
+        gather_terms(h * HA, HA, [(xa.at[R, 1, 1 + h], 0), (xa.at[L, 1, 1 + h], 0)])
     flush(phase)
-    for cp in [*near_a, *yra]:
-        cp.wait_recv()
-    for h in range(2):
-        acc = finish(h * HA, HA, [(xa.at[R, 1, 1 + h], 0), (xa.at[L, 1, 1 + h], 0), (ya.at[h], 0)], acc)
     yrb[0].wait_recv()
     for cp in (br1, bl1, br2, bl2):
         cp.wait_recv()
     for h in range(2):
         acc = finish(SA + h * HB, HB, [(yb.at[x], h * HB), (xb.at[R, 1 + h], 0), (xb.at[L, 1 + h], 0)], acc)
+    for h in range(2):
+        yra[h].wait_recv()
+        acc = finish_last(h * HA, HA, ya.at[h], acc)
     flush(rs)
     phase += [cp for cp in rs if id(cp) not in {id(e) for e in early}]
 

time: 160 us -> 159 us (level)
  no operation moved by 1% of the time
where the time goes in v5:
time: 159 us
  Pallas kernels  155 us (97%)
  local copies, waits for them, and re-layouts  3.1 us (2%)
    pallas_call x1, Pallas kernels, per_device(): pl.pallas_call(kernel, out_shape=(pltpu.VMEM((TOK, COLS), BF16), pltpu.VM...  155 us

profile of v5, /device:TPU:1, one launch (start us, length us, event | category | flops | bytes accessed | tf_op | source)
XLA Modules:
  0.0 158.8 jit_solution(17363165563137287105)
XLA Ops:
  0.6 0.0 copy-start
  0.6 0.7 copy-done
  1.3 155.0 %shard_map.59 = (bf16[768,1536]{1,0:T(8,128)(2,1)S(1)}, bf16[384,1536]{1,0:T(8,128)(2,1)S(1)}) custom-call(bf16[768,768]{1,0:T(8,128)(2,1)} %tok_hbm.1, bf16[768]{0:T(1024)(128)(2,1)S(1)} %copy-done, bf16[384,1536]{1,0:T(8,128)(2,1)} %w_hbm.1, bf16[1,6144,1536]{2,1,0:T(8,128)(2,1)} %grad_hbm.1), custom_call_target="tpu_custom_call" | custom-call | tf_op jit(solution)/shard_map/pallas_call | solution.py:516
  156.4 1.4 copy.8
  157.8 1.0 copy.9
Async XLA Ops:
  0.6 0.7 copy-start

commit v6 on v5

--- a/solution.py
+++ b/solution.py
@@ -539,7 +539,7 @@
             pltpu.SemaphoreType.DMA((11,)),
         ],
         compiler_params=pltpu.CompilerParams(
-            collective_id=0, has_side_effects=True, vmem_limit_bytes=50 * 1024 * 1024
+            collective_id=0, has_side_effects=True, vmem_limit_bytes=63500288
         ),
     )(tokens, ln_gain, weights, grad_partials)
 

time: 159 us -> 158 us (level)
  no operation moved by 1% of the time
where the time goes in v6:
time: 158 us
  Pallas kernels  155 us (98%)
  local copies, waits for them, and re-layouts  2.42 us (2%)
    pallas_call x1, Pallas kernels, per_device(): pl.pallas_call(kernel, out_shape=(pltpu.VMEM((TOK, COLS), BF16), pltpu.VM...  155 us

profile of v6, /device:TPU:1, one launch (start us, length us, event | category | flops | bytes accessed | tf_op | source)
XLA Modules:
  0.0 158.4 jit_solution(7803812504505473201)
XLA Ops:
  0.6 155.3 %shard_map.59 = (bf16[768,1536]{1,0:T(8,128)(2,1)S(1)}, bf16[384,1536]{1,0:T(8,128)(2,1)S(1)}) custom-call(bf16[768,768]{1,0:T(8,128)(2,1)} %tok_hbm.1, bf16[768]{0:T(1024)(128)(2,1)} %gain_hbm.1, bf16[384,1536]{1,0:T(8,128)(2,1)} %w_hbm.1, bf16[1,6144,1536]{2,1,0:T(8,128)(2,1)} %grad_hbm.1), custom_call_target="tpu_custom_call" | custom-call | tf_op jit(solution)/shard_map/pallas_call | solution.py:516
  156.0 1.4 copy.8
  157.4 1.0 copy.9

commit v7 on v6

--- a/solution.py
+++ b/solution.py
@@ -162,7 +162,7 @@
             pb[j, r, :] = v.astype(BF16)
             return 0
 
-        lax.fori_loop(0, n // CH, body, 0)
+        lax.fori_loop(0, n // CH, body, 0, unroll=3)
 
     def ready(key, first=0):
         if not first:
@@ -305,7 +305,7 @@
             gf[rows(r0 + i * CH, CH), :] = v
             return a + squared(v)
 
-        return lax.fori_loop(0, n // CH, body, acc)
+        return lax.fori_loop(0, n // CH, body, acc, unroll=3)
 
     def finish_last(r0, n, ref, acc):
         def body(i, a):
@@ -314,7 +314,7 @@
             gf[r, :] = v
             return a + squared(v)
 
-        return lax.fori_loop(0, n // CH, body, acc)
+        return lax.fori_loop(0, n // CH, body, acc, unroll=3)
 
     acc = jnp.zeros((8, 128), F32)
     phase = [*early, *(cp for cps in theirs.values() for cp in cps), ty, gy, *t1]
@@ -373,9 +373,9 @@
         j = block(xk, far)
         d2d.setdefault((xk, far, part), []).append(go(j, r0, n, core, c0, cn))
 
-    lax.fori_loop(GA // CH, BLK // CH, perturb, 0)
+    lax.fori_loop(GA // CH, BLK // CH, perturb, 0, unroll=2)
     ob = [go(jo, GA, GB, xdev[d]) for d in (R, L)]
-    lax.fori_loop(0, GA // CH, perturb, 0)
+    lax.fori_loop(0, GA // CH, perturb, 0, unroll=2)
     ya1 = go(jo, 0, GA, yfar)
     oa = [go(jo, 0, GA, xdev[d]) for d in (R, L)]
     across(0, False, 0, BLK)

time: 158 us -> 158 us (level)
  no operation moved by 1% of the time
where the time goes in v7:
time: 158 us
  Pallas kernels  155 us (98%)
  local copies, waits for them, and re-layouts  2.42 us (2%)
    pallas_call x1, Pallas kernels, per_device(): pl.pallas_call(kernel, out_shape=(pltpu.VMEM((TOK, COLS), BF16), pltpu.VM...  155 us

profile of v7, /device:TPU:1, one launch (start us, length us, event | category | flops | bytes accessed | tf_op | source)
XLA Modules:
  0.0 158.3 jit_solution(11820827559770071429)
XLA Ops:
  0.6 155.3 %shard_map.59 = (bf16[768,1536]{1,0:T(8,128)(2,1)S(1)}, bf16[384,1536]{1,0:T(8,128)(2,1)S(1)}) custom-call(bf16[768,768]{1,0:T(8,128)(2,1)} %tok_hbm.1, bf16[768]{0:T(1024)(128)(2,1)} %gain_hbm.1, bf16[384,1536]{1,0:T(8,128)(2,1)} %w_hbm.1, bf16[1,6144,1536]{2,1,0:T(8,128)(2,1)} %grad_hbm.1), custom_call_target="tpu_custom_call" | custom-call | tf_op jit(solution)/shard_map/pallas_call | solution.py:516
  155.9 1.4 copy.8
  157.3 1.0 copy.9
